TPU v7x, 32 devices: a whole 2x2x4 slice. The times are simulated.
32 devices in a mesh: sky: 4 (over x, core), tm: 8 (over z, y).
Axes of the slice: x: 2, y: 2, z: 4, core: 2. Of those that a mesh axis runs over, the one named last changes fastest.
Arguments:
- attitude: float32 [4, 8, 512], P(None, 'tm', 'sky'), may hold values from -6 to 6
- slot_time: float32 [262144], P(('sky', 'tm')), may hold values from -1 to 1
- slot_parallax: float32 [262144], P(('sky', 'tm')), may hold values from -1 to 1
- slot_observed: float32 [262144], P(('sky', 'tm')), may hold values from -6 to 6
- slot_phase: float32 [262144], P(('sky', 'tm')), may hold values from 0 to 1
- slot_knot: int32 [262144], P(('sky', 'tm')), may hold values from 0 to 508
- block_source: int32 [8192], P(('sky', 'tm')), may hold values from 0 to 63
- block_count: int32 [8192], P(('sky', 'tm')), may hold values from 1 to 32
- prior: float32 [5, 256], P(None, ('sky', 'tm')), may hold values from 0.5 to 4
Outputs:
- update: float32 [5, 256], P(None, ('sky', 'tm'))
Inputs may be any that keep to these rules, and one draw needn't show every extreme that they name: The four knots from slot_knot on lie in the transit's time group of 512 knots. `block_source`: an index into the 64 sources of the block's own sky sector.
All inputs are finite; a program needn't handle non-finite values.
Results may differ from a plain program's by a relative error of at most 0.0003.
Values sent between devices are 32-bit elements; how exact they have to be, the bound alone decides.
A program may use at most 64 MiB of HBM per device.

v0:
```python
import math
import jax
import jax.numpy as jnp
from jax import lax
from jax.sharding import PartitionSpec as P

PAIR_LIST = [(i, j) for i in range(5) for j in range(i, 5)]


def spline_quat(table, knot, phase):
    total = knot.shape[0]
    width = table.shape[1]
    step = math.gcd(total, 512)
    knot_rows = knot.reshape(total // step, step)
    phase_rows = phase.reshape(total // step, step)
    positions = jnp.arange(width, dtype=jnp.int32)

    def one_block(items):
        knot_here, phase_here = items
        weights = [
            (1.0 - phase_here) ** 3 / 6.0,
            (3.0 * phase_here**3 - 6.0 * phase_here**2 + 4.0) / 6.0,
            (-3.0 * phase_here**3 + 3.0 * phase_here**2 + 3.0 * phase_here + 1.0) / 6.0,
            phase_here**3 / 6.0,
        ]
        offset = positions[None, :] - knot_here[:, None]
        spread = jnp.zeros((step, width), jnp.float32)
        for i in range(4):
            spread = jnp.where(offset == i, weights[i][:, None], spread)
        return lax.dot_general(
            table,
            spread,
            (((1,), (1,)), ((), ())),
            precision=lax.Precision.HIGHEST,
            preferred_element_type=jnp.float32,
        )

    quat = lax.map(one_block, (knot_rows, phase_rows))
    return jnp.transpose(quat, (1, 0, 2)).reshape(4, total)


def block_sums(table, knot, phase, time, parallax, observed, count):
    quat = spline_quat(table, knot, phase)
    cross = quat[0] * quat[0] + quat[1] * quat[1] - quat[2] * quat[2] - quat[3] * quat[3]
    along = 2.0 * (quat[1] * quat[2] + quat[0] * quat[3])
    tilt = 2.0 * (quat[1] * quat[3] - quat[0] * quat[2])
    design = [cross, along, parallax, time * cross, time * along]
    residual = observed - tilt
    rows = [design[i] * design[j] for i, j in PAIR_LIST] + [design[i] * residual for i in range(5)]
    stacked = jnp.stack(rows)
    blocks = count.shape[0]
    stacked = stacked.reshape(20, blocks, -1)
    live = (jnp.arange(stacked.shape[2], dtype=jnp.int32)[None, :] < count[:, None]).astype(
        stacked.dtype
    )
    return jnp.sum(stacked * live[None], axis=2)


def source_sums(sums, block_source, sector_sources):
    blocks = block_source.shape[0]
    step = math.gcd(blocks, 512)
    source_rows = block_source.reshape(blocks // step, step)
    sum_rows = jnp.transpose(sums.reshape(20, blocks // step, step), (1, 0, 2))
    positions = jnp.arange(sector_sources, dtype=jnp.int32)

    def add_block(carry, items):
        source_here, sums_here = items
        member = (source_here[:, None] == positions[None, :]).astype(jnp.float32)
        return (
            carry
            + jnp.dot(
                sums_here,
                member,
                precision=lax.Precision.HIGHEST,
                preferred_element_type=jnp.float32,
            ),
            None,
        )

    start = jnp.zeros((20, sector_sources), jnp.float32)
    total, _ = lax.scan(add_block, start, (source_rows, sum_rows))
    return total


def solve_normals(normal, prior):
    entry = {}
    for index, pair in enumerate(PAIR_LIST):
        entry[pair[1], pair[0]] = normal[index]
    for i in range(5):
        entry[i, i] = entry[i, i] + prior[i]
    lower = {}
    for col in range(5):
        pivot = entry[col, col]
        for k in range(col):
            pivot = pivot - lower[col, k] * lower[col, k]
        root = jnp.sqrt(pivot)
        lower[col, col] = root
        for row in range(col + 1, 5):
            value = entry[row, col]
            for k in range(col):
                value = value - lower[row, k] * lower[col, k]
            lower[row, col] = value / root
    forward = []
    for i in range(5):
        value = normal[15 + i]
        for k in range(i):
            value = value - lower[i, k] * forward[k]
        forward.append(value / lower[i, i])
    result = [None] * 5
    for i in range(4, -1, -1):
        value = forward[i]
        for k in range(i + 1, 5):
            value = value - lower[k, i] * result[k]
        result[i] = value / lower[i, i]
    return jnp.stack(result)


def on_device(
    attitude,
    slot_time,
    slot_parallax,
    slot_observed,
    slot_phase,
    slot_knot,
    block_source,
    block_count,
    prior,
):
    group = lax.all_gather(attitude, "sky", axis=2, tiled=True)
    table = group[:, 0, :]
    sums = block_sums(
        table, slot_knot, slot_phase, slot_time, slot_parallax, slot_observed, block_count
    )
    owned = prior.shape[1]
    sector_sources = owned * lax.axis_size("tm")
    partial_value = source_sums(sums, block_source, sector_sources)
    total = lax.psum(partial_value, "tm")
    normal = lax.dynamic_slice_in_dim(total, lax.axis_index("tm") * owned, owned, 1)
    return solve_normals(normal, prior)


def solution(mesh):
    in_specs = (
        P(None, "tm", "sky"),
        P(("sky", "tm")),
        P(("sky", "tm")),
        P(("sky", "tm")),
        P(("sky", "tm")),
        P(("sky", "tm")),
        P(("sky", "tm")),
        P(("sky", "tm")),
        P(None, ("sky", "tm")),
    )
    out_specs = P(None, ("sky", "tm"))
    return jax.shard_map(
        on_device, mesh=mesh, in_specs=in_specs, out_specs=out_specs, check_vma=False
    )
```

profile of v0, /device:TPU:0, one launch (start us, length us, event | category | flops | bytes accessed | tf_op | source)
XLA Modules:
  0.0 77.9 jit_solution(18191354367063263991)
XLA Ops:
  0.0 0.8 reshape.292
  0.8 0.7 copy-done.4
  1.5 6.2 %all_gather.3 = f32[4,1,512]{2,0,1:T(4,128)S(1)} all-gather(f32[4,1,128]{2,0,1:T(4,128)S(1)} %bitcast.33), channel_id=1, replica_groups=mesh['sky'=4,'tm'=8] {'sky'}, dimensions={2}, use_global_device_ids=true | all-gather | bytes 10240 | tf_op jit(solution)/shard_map/all_gather | solution.py:129
  7.6 22.9 %while.3 = (s32[]{:T(128)}, f32[16,4,512]{2,1,0:T(4,128)S(1)}, s32[16,512]{1,0:T(8,128)S(1)}, f32[16,512]{1,0:T(8,128)S(1)}, f32[4,512]{1,0:T(4,128)S(1)}, /*index=5*/s32[]{:T(128)}) while((s32[]{:T(128)}, f32[16,4,512]{2,1,0:T(4,128)S(1)}, s32[16,512]{1,0:T(8,128)S(1)}, f32[16,512]{1,0:T(8,128)S(1)}, f32[4,512]{1,0:T(4,128)S(1)}, ...), condition=%wide.region_1.2_spmd.clone, body=%wide.region_0.1_spmd.clone.sunk | while | flops 14951938 | bytes 45145 | solution.py:38
  7.6 1.4 %fusion.59 = f32[16,4,512]{2,1,0:T(4,128)S(1)} fusion(f32[16,4,512]{2,1,0:T(4,128)S(1)} %get-tuple-element.192, s32[]{:T(128)S(6)} %copy.59, f32[4,512]{1,0:T(4,128)S(1)} %get-tuple-element.201, f32[512]{0:T(512)S(1)} %get-tuple-element.181, f32[512]{0:T(512)S(1)} %get-tuple-element.182, f32[512]{0:T(512)S(1)} %get-tuple-element.183, ...), kind=kOutput, calls=%fused_computation.2.clone.1 | convolution fusion | flops 14942208 | bytes 26628 | tf_op jit(solution)/shard_map/while/body/eval_jaxpr/dot_general | solution.py:30
  9.1 1.4 %fusion.59 = f32[16,4,512]{2,1,0:T(4,128)S(1)} fusion(f32[16,4,512]{2,1,0:T(4,128)S(1)} %get-tuple-element.192, s32[]{:T(128)S(6)} %copy.59, f32[4,512]{1,0:T(4,128)S(1)} %get-tuple-element.201, f32[512]{0:T(512)S(1)} %get-tuple-element.181, f32[512]{0:T(512)S(1)} %get-tuple-element.182, f32[512]{0:T(512)S(1)} %get-tuple-element.183, ...), kind=kOutput, calls=%fused_computation.2.clone.1 | convolution fusion | flops 14942208 | bytes 26628 | tf_op jit(solution)/shard_map/while/body/eval_jaxpr/dot_general | solution.py:30
  10.5 1.4 %fusion.59 = f32[16,4,512]{2,1,0:T(4,128)S(1)} fusion(f32[16,4,512]{2,1,0:T(4,128)S(1)} %get-tuple-element.192, s32[]{:T(128)S(6)} %copy.59, f32[4,512]{1,0:T(4,128)S(1)} %get-tuple-element.201, f32[512]{0:T(512)S(1)} %get-tuple-element.181, f32[512]{0:T(512)S(1)} %get-tuple-element.182, f32[512]{0:T(512)S(1)} %get-tuple-element.183, ...), kind=kOutput, calls=%fused_computation.2.clone.1 | convolution fusion | flops 14942208 | bytes 26628 | tf_op jit(solution)/shard_map/while/body/eval_jaxpr/dot_general | solution.py:30
  12.0 1.4 %fusion.59 = f32[16,4,512]{2,1,0:T(4,128)S(1)} fusion(f32[16,4,512]{2,1,0:T(4,128)S(1)} %get-tuple-element.192, s32[]{:T(128)S(6)} %copy.59, f32[4,512]{1,0:T(4,128)S(1)} %get-tuple-element.201, f32[512]{0:T(512)S(1)} %get-tuple-element.181, f32[512]{0:T(512)S(1)} %get-tuple-element.182, f32[512]{0:T(512)S(1)} %get-tuple-element.183, ...), kind=kOutput, calls=%fused_computation.2.clone.1 | convolution fusion | flops 14942208 | bytes 26628 | tf_op jit(solution)/shard_map/while/body/eval_jaxpr/dot_general | solution.py:30
  13.4 1.4 %fusion.59 = f32[16,4,512]{2,1,0:T(4,128)S(1)} fusion(f32[16,4,512]{2,1,0:T(4,128)S(1)} %get-tuple-element.192, s32[]{:T(128)S(6)} %copy.59, f32[4,512]{1,0:T(4,128)S(1)} %get-tuple-element.201, f32[512]{0:T(512)S(1)} %get-tuple-element.181, f32[512]{0:T(512)S(1)} %get-tuple-element.182, f32[512]{0:T(512)S(1)} %get-tuple-element.183, ...), kind=kOutput, calls=%fused_computation.2.clone.1 | convolution fusion | flops 14942208 | bytes 26628 | tf_op jit(solution)/shard_map/while/body/eval_jaxpr/dot_general | solution.py:30
  14.8 1.4 %fusion.59 = f32[16,4,512]{2,1,0:T(4,128)S(1)} fusion(f32[16,4,512]{2,1,0:T(4,128)S(1)} %get-tuple-element.192, s32[]{:T(128)S(6)} %copy.59, f32[4,512]{1,0:T(4,128)S(1)} %get-tuple-element.201, f32[512]{0:T(512)S(1)} %get-tuple-element.181, f32[512]{0:T(512)S(1)} %get-tuple-element.182, f32[512]{0:T(512)S(1)} %get-tuple-element.183, ...), kind=kOutput, calls=%fused_computation.2.clone.1 | convolution fusion | flops 14942208 | bytes 26628 | tf_op jit(solution)/shard_map/while/body/eval_jaxpr/dot_general | solution.py:30
  16.3 1.4 %fusion.59 = f32[16,4,512]{2,1,0:T(4,128)S(1)} fusion(f32[16,4,512]{2,1,0:T(4,128)S(1)} %get-tuple-element.192, s32[]{:T(128)S(6)} %copy.59, f32[4,512]{1,0:T(4,128)S(1)} %get-tuple-element.201, f32[512]{0:T(512)S(1)} %get-tuple-element.181, f32[512]{0:T(512)S(1)} %get-tuple-element.182, f32[512]{0:T(512)S(1)} %get-tuple-element.183, ...), kind=kOutput, calls=%fused_computation.2.clone.1 | convolution fusion | flops 14942208 | bytes 26628 | tf_op jit(solution)/shard_map/while/body/eval_jaxpr/dot_general | solution.py:30
  17.7 1.4 %fusion.59 = f32[16,4,512]{2,1,0:T(4,128)S(1)} fusion(f32[16,4,512]{2,1,0:T(4,128)S(1)} %get-tuple-element.192, s32[]{:T(128)S(6)} %copy.59, f32[4,512]{1,0:T(4,128)S(1)} %get-tuple-element.201, f32[512]{0:T(512)S(1)} %get-tuple-element.181, f32[512]{0:T(512)S(1)} %get-tuple-element.182, f32[512]{0:T(512)S(1)} %get-tuple-element.183, ...), kind=kOutput, calls=%fused_computation.2.clone.1 | convolution fusion | flops 14942208 | bytes 26628 | tf_op jit(solution)/shard_map/while/body/eval_jaxpr/dot_general | solution.py:30
  19.1 1.4 %fusion.59 = f32[16,4,512]{2,1,0:T(4,128)S(1)} fusion(f32[16,4,512]{2,1,0:T(4,128)S(1)} %get-tuple-element.192, s32[]{:T(128)S(6)} %copy.59, f32[4,512]{1,0:T(4,128)S(1)} %get-tuple-element.201, f32[512]{0:T(512)S(1)} %get-tuple-element.181, f32[512]{0:T(512)S(1)} %get-tuple-element.182, f32[512]{0:T(512)S(1)} %get-tuple-element.183, ...), kind=kOutput, calls=%fused_computation.2.clone.1 | convolution fusion | flops 14942208 | bytes 26628 | tf_op jit(solution)/shard_map/while/body/eval_jaxpr/dot_general | solution.py:30
  20.6 1.4 %fusion.59 = f32[16,4,512]{2,1,0:T(4,128)S(1)} fusion(f32[16,4,512]{2,1,0:T(4,128)S(1)} %get-tuple-element.192, s32[]{:T(128)S(6)} %copy.59, f32[4,512]{1,0:T(4,128)S(1)} %get-tuple-element.201, f32[512]{0:T(512)S(1)} %get-tuple-element.181, f32[512]{0:T(512)S(1)} %get-tuple-element.182, f32[512]{0:T(512)S(1)} %get-tuple-element.183, ...), kind=kOutput, calls=%fused_computation.2.clone.1 | convolution fusion | flops 14942208 | bytes 26628 | tf_op jit(solution)/shard_map/while/body/eval_jaxpr/dot_general | solution.py:30
  22.0 1.4 %fusion.59 = f32[16,4,512]{2,1,0:T(4,128)S(1)} fusion(f32[16,4,512]{2,1,0:T(4,128)S(1)} %get-tuple-element.192, s32[]{:T(128)S(6)} %copy.59, f32[4,512]{1,0:T(4,128)S(1)} %get-tuple-element.201, f32[512]{0:T(512)S(1)} %get-tuple-element.181, f32[512]{0:T(512)S(1)} %get-tuple-element.182, f32[512]{0:T(512)S(1)} %get-tuple-element.183, ...), kind=kOutput, calls=%fused_computation.2.clone.1 | convolution fusion | flops 14942208 | bytes 26628 | tf_op jit(solution)/shard_map/while/body/eval_jaxpr/dot_general | solution.py:30
  23.4 1.4 %fusion.59 = f32[16,4,512]{2,1,0:T(4,128)S(1)} fusion(f32[16,4,512]{2,1,0:T(4,128)S(1)} %get-tuple-element.192, s32[]{:T(128)S(6)} %copy.59, f32[4,512]{1,0:T(4,128)S(1)} %get-tuple-element.201, f32[512]{0:T(512)S(1)} %get-tuple-element.181, f32[512]{0:T(512)S(1)} %get-tuple-element.182, f32[512]{0:T(512)S(1)} %get-tuple-element.183, ...), kind=kOutput, calls=%fused_computation.2.clone.1 | convolution fusion | flops 14942208 | bytes 26628 | tf_op jit(solution)/shard_map/while/body/eval_jaxpr/dot_general | solution.py:30
  24.9 1.4 %fusion.59 = f32[16,4,512]{2,1,0:T(4,128)S(1)} fusion(f32[16,4,512]{2,1,0:T(4,128)S(1)} %get-tuple-element.192, s32[]{:T(128)S(6)} %copy.59, f32[4,512]{1,0:T(4,128)S(1)} %get-tuple-element.201, f32[512]{0:T(512)S(1)} %get-tuple-element.181, f32[512]{0:T(512)S(1)} %get-tuple-element.182, f32[512]{0:T(512)S(1)} %get-tuple-element.183, ...), kind=kOutput, calls=%fused_computation.2.clone.1 | convolution fusion | flops 14942208 | bytes 26628 | tf_op jit(solution)/shard_map/while/body/eval_jaxpr/dot_general | solution.py:30
  26.3 1.4 %fusion.59 = f32[16,4,512]{2,1,0:T(4,128)S(1)} fusion(f32[16,4,512]{2,1,0:T(4,128)S(1)} %get-tuple-element.192, s32[]{:T(128)S(6)} %copy.59, f32[4,512]{1,0:T(4,128)S(1)} %get-tuple-element.201, f32[512]{0:T(512)S(1)} %get-tuple-element.181, f32[512]{0:T(512)S(1)} %get-tuple-element.182, f32[512]{0:T(512)S(1)} %get-tuple-element.183, ...), kind=kOutput, calls=%fused_computation.2.clone.1 | convolution fusion | flops 14942208 | bytes 26628 | tf_op jit(solution)/shard_map/while/body/eval_jaxpr/dot_general | solution.py:30
  27.7 1.4 %fusion.59 = f32[16,4,512]{2,1,0:T(4,128)S(1)} fusion(f32[16,4,512]{2,1,0:T(4,128)S(1)} %get-tuple-element.192, s32[]{:T(128)S(6)} %copy.59, f32[4,512]{1,0:T(4,128)S(1)} %get-tuple-element.201, f32[512]{0:T(512)S(1)} %get-tuple-element.181, f32[512]{0:T(512)S(1)} %get-tuple-element.182, f32[512]{0:T(512)S(1)} %get-tuple-element.183, ...), kind=kOutput, calls=%fused_computation.2.clone.1 | convolution fusion | flops 14942208 | bytes 26628 | tf_op jit(solution)/shard_map/while/body/eval_jaxpr/dot_general | solution.py:30
  29.2 1.4 %fusion.59 = f32[16,4,512]{2,1,0:T(4,128)S(1)} fusion(f32[16,4,512]{2,1,0:T(4,128)S(1)} %get-tuple-element.192, s32[]{:T(128)S(6)} %copy.59, f32[4,512]{1,0:T(4,128)S(1)} %get-tuple-element.201, f32[512]{0:T(512)S(1)} %get-tuple-element.181, f32[512]{0:T(512)S(1)} %get-tuple-element.182, f32[512]{0:T(512)S(1)} %get-tuple-element.183, ...), kind=kOutput, calls=%fused_computation.2.clone.1 | convolution fusion | flops 14942208 | bytes 26628 | tf_op jit(solution)/shard_map/while/body/eval_jaxpr/dot_general | solution.py:30
  30.5 0.4 multiply_reduce_fusion.1
  31.0 0.1 reshape.294
  31.2 0.1 reshape.295
  31.3 0.7 copy-done
  32.1 0.7 copy-done.1
  32.9 0.1 stack.65
  33.0 0.1 copy.27
  33.1 0.1 stack.66
  33.2 0.1 copy.28
  33.3 0.1 stack.67
  33.4 0.1 copy.29
  33.5 0.1 reshape.296
  33.6 0.1 stack.68
  33.7 0.1 copy.31
  33.8 0.1 stack.69
  33.9 0.1 copy.32
  34.0 0.1 stack.70
  34.2 0.1 stack.71
  34.4 0.1 stack.72
  34.5 0.1 stack.73
  34.7 0.1 stack.74
  34.9 0.1 stack.75
  35.1 0.1 stack.76
  35.3 0.1 stack.77
  35.4 0.1 stack.78
  35.6 0.1 stack.79
  35.8 0.1 stack.80
  36.0 0.1 stack.81
  36.2 0.7 copy-done.6
  36.8 0.1 multiply_reduce_fusion
  36.9 0.6 copy-done.7
  37.5 0.3 fusion.39
  37.9 37.9 %psum.7 = f32[20,64]{0,1:T(8,128)S(1)} all-reduce(f32[20,64]{0,1:T(8,128)S(1)} %fusion.39), channel_id=1, replica_groups=mesh['sky'=4,'tm'=8] {'tm'}, use_global_device_ids=true, to_apply=%region_3.4 | all-reduce | flops 1280 | bytes 10240 | tf_op jit(solution)/shard_map/psum | solution.py:137
  75.8 0.7 copy-done.5
  76.5 0.1 copy.54
  76.5 0.1 copy.53
  76.6 0.1 copy.52
  76.7 0.1 copy.51
  76.8 0.1 subtract_divide_fusion.7
  76.9 0.1 subtract_divide_fusion.4
  77.0 0.1 copy.55
  77.1 0.1 subtract_divide_fusion
  77.2 0.1 stack.83
  77.3 0.7 copy.50
  (101 shorter events, 2.0 us)
Async XLA Ops:
  0.0 0.8 copy-start.3
  0.8 0.7 copy-start.4
  31.3 0.8 copy-start
  31.3 0.8 %copy-start.2 = (f32[8192]{0:T(1024)S(1)}, f32[8192]{0:T(1024)}, u32[]{:S(2)}) copy-start(f32[8192]{0:T(1024)} %param.14) | copy-start | bytes 98308
  32.1 0.8 copy-start.1
  36.1 0.7 copy-start.6
  36.8 0.7 copy-start.7
  75.8 0.7 copy-start.5
where the time goes:
time: 78.4 us; the launch traced here: 77.9 us
  blocking collectives  44.1 us (56%)
  matrix products  22.3 us (28%)
  local copies, waits for them, and re-layouts  9.75 us (12%)
  other arithmetic  1.07 us (1%)
    psum x1, blocking collectives, on_device(): total = lax.psum(partial_value, 'tm')  37.9 us
    dot_general x16, matrix products, one_block(): lax.dot_general(table, spread, (((1,), (1,)), ((), ())), precision=lax.Pr...  22 us
    all_gather x1, blocking collectives, on_device(): group = lax.all_gather(attitude, 'sky', axis=2, tiled=True)  6.15 us
    unnamed x40, local copies, waits for them, and re-layouts  4.73 us
    another operation x35, local copies, waits for them, and re-layouts, block_sums(): stacked = jnp.stack(rows)  2.6 us

commit v1 on v0

--- a/solution.py
+++ b/solution.py
@@ -134,7 +134,9 @@
     owned = prior.shape[1]
     sector_sources = owned * lax.axis_size("tm")
     partial_value = source_sums(sums, block_source, sector_sources)
-    total = lax.psum(partial_value, "tm")
+    total = partial_value
+    for hop in (1, 2, 4):
+        total = total + lax.ppermute(total, "tm", [(dev, dev ^ hop) for dev in range(8)])
     normal = lax.dynamic_slice_in_dim(total, lax.axis_index("tm") * owned, owned, 1)
     return solve_normals(normal, prior)
 

time: 78.4 us -> 51.2 us (0.65)
  blocking collectives: 44.1 us -> 6.15 us
  starting transfers between devices: 0 us -> 7.2 us
  waiting for transfers between devices: 0 us -> 5.02 us
  local copies, waits for them, and re-layouts: 9.75 us -> 8.47 us
    psum x1 -> x0, blocking collectives: 37.9 us -> none  [on_device(): total = lax.psum(partial_value, 'tm')]
    ppermute x0 -> x3, starting transfers between devices: none -> 7.2 us  [on_device(): lax.ppermute(total, 'tm', [(dev, dev ^ hop) for dev in range(8)])]
    ppermute x0 -> x3, waiting for transfers between devices: none -> 5.02 us  [on_device(): lax.ppermute(total, 'tm', [(dev, dev ^ hop) for dev in range(8)])]
    unnamed x40 -> x35, local copies, waits for them, and re-layouts: 4.73 us -> 3.41 us
  transfers between devices with their start and end apart: 0 -> 3, of which waited for: 0 -> 3; matrix products, arithmetic and copies ran while one was open for 0% -> 0% of each run, Pallas kernels for 0% -> 0%
where the time goes in v1:
time: 51.2 us; the launch traced here: 50.8 us
  matrix products  22.2 us (43%)
  local copies, waits for them, and re-layouts  8.47 us (17%)
  starting transfers between devices  7.2 us (14%)
  blocking collectives  6.15 us (12%)
  waiting for transfers between devices  5.02 us (10%)
  other arithmetic  0.97 us (2%)
    dot_general x16, matrix products, one_block(): lax.dot_general(table, spread, (((1,), (1,)), ((), ())), precision=lax.Pr...  22 us
    ppermute x3, starting transfers between devices, on_device(): lax.ppermute(total, 'tm', [(dev, dev ^ hop) for dev in range(8)])  7.2 us
    all_gather x1, blocking collectives, on_device(): group = lax.all_gather(attitude, 'sky', axis=2, tiled=True)  6.15 us
    ppermute x3, waiting for transfers between devices, on_device(): lax.ppermute(total, 'tm', [(dev, dev ^ hop) for dev in range(8)])  5.02 us
    unnamed x35, local copies, waits for them, and re-layouts  3.41 us
    another operation x35, local copies, waits for them, and re-layouts, block_sums(): stacked = jnp.stack(rows)  2.78 us
  transfers between devices with their start and end apart: 3, of which 3 were waited for; matrix products, arithmetic and copies ran while one was open for 0% of the time, Pallas kernels for 0%

profile of v1, /device:TPU:0, one launch (start us, length us, event | category | flops | bytes accessed | tf_op | source)
XLA Modules:
  0.0 50.8 jit_solution(14085658820670353)
XLA Ops:
  0.0 0.8 %reshape.292 = s32[16,512]{1,0:T(8,128)S(1)} reshape(s32[8192]{0:T(1024)} %param.16) | data formatting | bytes 65536 | tf_op jit(solution)/shard_map/reshape | solution.py:14
  0.8 0.7 %copy-done.5 = f32[4,1,128]{2,1,0:T(1,128)S(1)} copy-done((f32[4,1,128]{2,1,0:T(1,128)S(1)}, f32[4,1,128]{2,1,0:T(1,128)}, u32[]{:S(2)}) %copy-start.5) | copy-done | bytes 2072
  1.5 6.2 %all_gather.3 = f32[4,1,512]{2,0,1:T(4,128)S(1)} all-gather(f32[4,1,128]{2,0,1:T(4,128)S(1)} %bitcast.33), channel_id=1, replica_groups=mesh['sky'=4,'tm'=8] {'sky'}, dimensions={2}, use_global_device_ids=true | all-gather | bytes 10240 | tf_op jit(solution)/shard_map/all_gather | solution.py:129
  7.6 22.9 %while.3 = (s32[]{:T(128)}, f32[16,4,512]{2,1,0:T(4,128)S(1)}, s32[16,512]{1,0:T(8,128)S(1)}, f32[16,512]{1,0:T(8,128)S(1)}, f32[4,512]{1,0:T(4,128)S(1)}, /*index=5*/s32[]{:T(128)}) while((s32[]{:T(128)}, f32[16,4,512]{2,1,0:T(4,128)S(1)}, s32[16,512]{1,0:T(8,128)S(1)}, f32[16,512]{1,0:T(8,128)S(1)}, f32[4,512]{1,0:T(4,128)S(1)}, ...), condition=%wide.region_1.2_spmd.clone, body=%wide.region_0.1_spmd.clone.sunk | while | flops 14951938 | bytes 45145 | solution.py:38
  7.6 1.4 %fusion.93 = f32[16,4,512]{2,1,0:T(4,128)S(1)} fusion(f32[16,4,512]{2,1,0:T(4,128)S(1)} %get-tuple-element.186, s32[]{:T(128)S(6)} %copy.36, f32[4,512]{1,0:T(4,128)S(1)} %get-tuple-element.195, f32[512]{0:T(512)S(1)} %get-tuple-element.175, f32[512]{0:T(512)S(1)} %get-tuple-element.176, f32[512]{0:T(512)S(1)} %get-tuple-element.177, ...), kind=kOutput, calls=%fused_computation.2.clone.1 | convolution fusion | flops 14942208 | bytes 26628 | tf_op jit(solution)/shard_map/while/body/eval_jaxpr/dot_general | solution.py:30
  9.1 1.4 %fusion.93 = f32[16,4,512]{2,1,0:T(4,128)S(1)} fusion(f32[16,4,512]{2,1,0:T(4,128)S(1)} %get-tuple-element.186, s32[]{:T(128)S(6)} %copy.36, f32[4,512]{1,0:T(4,128)S(1)} %get-tuple-element.195, f32[512]{0:T(512)S(1)} %get-tuple-element.175, f32[512]{0:T(512)S(1)} %get-tuple-element.176, f32[512]{0:T(512)S(1)} %get-tuple-element.177, ...), kind=kOutput, calls=%fused_computation.2.clone.1 | convolution fusion | flops 14942208 | bytes 26628 | tf_op jit(solution)/shard_map/while/body/eval_jaxpr/dot_general | solution.py:30
  10.5 1.4 %fusion.93 = f32[16,4,512]{2,1,0:T(4,128)S(1)} fusion(f32[16,4,512]{2,1,0:T(4,128)S(1)} %get-tuple-element.186, s32[]{:T(128)S(6)} %copy.36, f32[4,512]{1,0:T(4,128)S(1)} %get-tuple-element.195, f32[512]{0:T(512)S(1)} %get-tuple-element.175, f32[512]{0:T(512)S(1)} %get-tuple-element.176, f32[512]{0:T(512)S(1)} %get-tuple-element.177, ...), kind=kOutput, calls=%fused_computation.2.clone.1 | convolution fusion | flops 14942208 | bytes 26628 | tf_op jit(solution)/shard_map/while/body/eval_jaxpr/dot_general | solution.py:30
  11.9 1.4 %fusion.93 = f32[16,4,512]{2,1,0:T(4,128)S(1)} fusion(f32[16,4,512]{2,1,0:T(4,128)S(1)} %get-tuple-element.186, s32[]{:T(128)S(6)} %copy.36, f32[4,512]{1,0:T(4,128)S(1)} %get-tuple-element.195, f32[512]{0:T(512)S(1)} %get-tuple-element.175, f32[512]{0:T(512)S(1)} %get-tuple-element.176, f32[512]{0:T(512)S(1)} %get-tuple-element.177, ...), kind=kOutput, calls=%fused_computation.2.clone.1 | convolution fusion | flops 14942208 | bytes 26628 | tf_op jit(solution)/shard_map/while/body/eval_jaxpr/dot_general | solution.py:30
  13.4 1.4 %fusion.93 = f32[16,4,512]{2,1,0:T(4,128)S(1)} fusion(f32[16,4,512]{2,1,0:T(4,128)S(1)} %get-tuple-element.186, s32[]{:T(128)S(6)} %copy.36, f32[4,512]{1,0:T(4,128)S(1)} %get-tuple-element.195, f32[512]{0:T(512)S(1)} %get-tuple-element.175, f32[512]{0:T(512)S(1)} %get-tuple-element.176, f32[512]{0:T(512)S(1)} %get-tuple-element.177, ...), kind=kOutput, calls=%fused_computation.2.clone.1 | convolution fusion | flops 14942208 | bytes 26628 | tf_op jit(solution)/shard_map/while/body/eval_jaxpr/dot_general | solution.py:30
  14.8 1.4 %fusion.93 = f32[16,4,512]{2,1,0:T(4,128)S(1)} fusion(f32[16,4,512]{2,1,0:T(4,128)S(1)} %get-tuple-element.186, s32[]{:T(128)S(6)} %copy.36, f32[4,512]{1,0:T(4,128)S(1)} %get-tuple-element.195, f32[512]{0:T(512)S(1)} %get-tuple-element.175, f32[512]{0:T(512)S(1)} %get-tuple-element.176, f32[512]{0:T(512)S(1)} %get-tuple-element.177, ...), kind=kOutput, calls=%fused_computation.2.clone.1 | convolution fusion | flops 14942208 | bytes 26628 | tf_op jit(solution)/shard_map/while/body/eval_jaxpr/dot_general | solution.py:30
  16.2 1.4 %fusion.93 = f32[16,4,512]{2,1,0:T(4,128)S(1)} fusion(f32[16,4,512]{2,1,0:T(4,128)S(1)} %get-tuple-element.186, s32[]{:T(128)S(6)} %copy.36, f32[4,512]{1,0:T(4,128)S(1)} %get-tuple-element.195, f32[512]{0:T(512)S(1)} %get-tuple-element.175, f32[512]{0:T(512)S(1)} %get-tuple-element.176, f32[512]{0:T(512)S(1)} %get-tuple-element.177, ...), kind=kOutput, calls=%fused_computation.2.clone.1 | convolution fusion | flops 14942208 | bytes 26628 | tf_op jit(solution)/shard_map/while/body/eval_jaxpr/dot_general | solution.py:30
  17.7 1.4 %fusion.93 = f32[16,4,512]{2,1,0:T(4,128)S(1)} fusion(f32[16,4,512]{2,1,0:T(4,128)S(1)} %get-tuple-element.186, s32[]{:T(128)S(6)} %copy.36, f32[4,512]{1,0:T(4,128)S(1)} %get-tuple-element.195, f32[512]{0:T(512)S(1)} %get-tuple-element.175, f32[512]{0:T(512)S(1)} %get-tuple-element.176, f32[512]{0:T(512)S(1)} %get-tuple-element.177, ...), kind=kOutput, calls=%fused_computation.2.clone.1 | convolution fusion | flops 14942208 | bytes 26628 | tf_op jit(solution)/shard_map/while/body/eval_jaxpr/dot_general | solution.py:30
  19.1 1.4 %fusion.93 = f32[16,4,512]{2,1,0:T(4,128)S(1)} fusion(f32[16,4,512]{2,1,0:T(4,128)S(1)} %get-tuple-element.186, s32[]{:T(128)S(6)} %copy.36, f32[4,512]{1,0:T(4,128)S(1)} %get-tuple-element.195, f32[512]{0:T(512)S(1)} %get-tuple-element.175, f32[512]{0:T(512)S(1)} %get-tuple-element.176, f32[512]{0:T(512)S(1)} %get-tuple-element.177, ...), kind=kOutput, calls=%fused_computation.2.clone.1 | convolution fusion | flops 14942208 | bytes 26628 | tf_op jit(solution)/shard_map/while/body/eval_jaxpr/dot_general | solution.py:30
  20.5 1.4 %fusion.93 = f32[16,4,512]{2,1,0:T(4,128)S(1)} fusion(f32[16,4,512]{2,1,0:T(4,128)S(1)} %get-tuple-element.186, s32[]{:T(128)S(6)} %copy.36, f32[4,512]{1,0:T(4,128)S(1)} %get-tuple-element.195, f32[512]{0:T(512)S(1)} %get-tuple-element.175, f32[512]{0:T(512)S(1)} %get-tuple-element.176, f32[512]{0:T(512)S(1)} %get-tuple-element.177, ...), kind=kOutput, calls=%fused_computation.2.clone.1 | convolution fusion | flops 14942208 | bytes 26628 | tf_op jit(solution)/shard_map/while/body/eval_jaxpr/dot_general | solution.py:30
  22.0 1.4 %fusion.93 = f32[16,4,512]{2,1,0:T(4,128)S(1)} fusion(f32[16,4,512]{2,1,0:T(4,128)S(1)} %get-tuple-element.186, s32[]{:T(128)S(6)} %copy.36, f32[4,512]{1,0:T(4,128)S(1)} %get-tuple-element.195, f32[512]{0:T(512)S(1)} %get-tuple-element.175, f32[512]{0:T(512)S(1)} %get-tuple-element.176, f32[512]{0:T(512)S(1)} %get-tuple-element.177, ...), kind=kOutput, calls=%fused_computation.2.clone.1 | convolution fusion | flops 14942208 | bytes 26628 | tf_op jit(solution)/shard_map/while/body/eval_jaxpr/dot_general | solution.py:30
  23.4 1.4 %fusion.93 = f32[16,4,512]{2,1,0:T(4,128)S(1)} fusion(f32[16,4,512]{2,1,0:T(4,128)S(1)} %get-tuple-element.186, s32[]{:T(128)S(6)} %copy.36, f32[4,512]{1,0:T(4,128)S(1)} %get-tuple-element.195, f32[512]{0:T(512)S(1)} %get-tuple-element.175, f32[512]{0:T(512)S(1)} %get-tuple-element.176, f32[512]{0:T(512)S(1)} %get-tuple-element.177, ...), kind=kOutput, calls=%fused_computation.2.clone.1 | convolution fusion | flops 14942208 | bytes 26628 | tf_op jit(solution)/shard_map/while/body/eval_jaxpr/dot_general | solution.py:30
  24.8 1.4 %fusion.93 = f32[16,4,512]{2,1,0:T(4,128)S(1)} fusion(f32[16,4,512]{2,1,0:T(4,128)S(1)} %get-tuple-element.186, s32[]{:T(128)S(6)} %copy.36, f32[4,512]{1,0:T(4,128)S(1)} %get-tuple-element.195, f32[512]{0:T(512)S(1)} %get-tuple-element.175, f32[512]{0:T(512)S(1)} %get-tuple-element.176, f32[512]{0:T(512)S(1)} %get-tuple-element.177, ...), kind=kOutput, calls=%fused_computation.2.clone.1 | convolution fusion | flops 14942208 | bytes 26628 | tf_op jit(solution)/shard_map/while/body/eval_jaxpr/dot_general | solution.py:30
  26.3 1.4 %fusion.93 = f32[16,4,512]{2,1,0:T(4,128)S(1)} fusion(f32[16,4,512]{2,1,0:T(4,128)S(1)} %get-tuple-element.186, s32[]{:T(128)S(6)} %copy.36, f32[4,512]{1,0:T(4,128)S(1)} %get-tuple-element.195, f32[512]{0:T(512)S(1)} %get-tuple-element.175, f32[512]{0:T(512)S(1)} %get-tuple-element.176, f32[512]{0:T(512)S(1)} %get-tuple-element.177, ...), kind=kOutput, calls=%fused_computation.2.clone.1 | convolution fusion | flops 14942208 | bytes 26628 | tf_op jit(solution)/shard_map/while/body/eval_jaxpr/dot_general | solution.py:30
  27.7 1.4 %fusion.93 = f32[16,4,512]{2,1,0:T(4,128)S(1)} fusion(f32[16,4,512]{2,1,0:T(4,128)S(1)} %get-tuple-element.186, s32[]{:T(128)S(6)} %copy.36, f32[4,512]{1,0:T(4,128)S(1)} %get-tuple-element.195, f32[512]{0:T(512)S(1)} %get-tuple-element.175, f32[512]{0:T(512)S(1)} %get-tuple-element.176, f32[512]{0:T(512)S(1)} %get-tuple-element.177, ...), kind=kOutput, calls=%fused_computation.2.clone.1 | convolution fusion | flops 14942208 | bytes 26628 | tf_op jit(solution)/shard_map/while/body/eval_jaxpr/dot_general | solution.py:30
  29.1 1.4 %fusion.93 = f32[16,4,512]{2,1,0:T(4,128)S(1)} fusion(f32[16,4,512]{2,1,0:T(4,128)S(1)} %get-tuple-element.186, s32[]{:T(128)S(6)} %copy.36, f32[4,512]{1,0:T(4,128)S(1)} %get-tuple-element.195, f32[512]{0:T(512)S(1)} %get-tuple-element.175, f32[512]{0:T(512)S(1)} %get-tuple-element.176, f32[512]{0:T(512)S(1)} %get-tuple-element.177, ...), kind=kOutput, calls=%fused_computation.2.clone.1 | convolution fusion | flops 14942208 | bytes 26628 | tf_op jit(solution)/shard_map/while/body/eval_jaxpr/dot_general | solution.py:30
  30.5 0.4 multiply_reduce_fusion.1
  31.0 0.1 reshape.294
  31.1 0.1 reshape.295
  31.3 0.7 %copy-done = f32[8192]{0:T(1024)S(1)} copy-done((f32[8192]{0:T(1024)S(1)}, f32[8192]{0:T(1024)}, u32[]{:S(2)}) %copy-start) | copy-done | bytes 32792
  32.0 0.7 %copy-done.1 = f32[8192]{0:T(1024)S(1)} copy-done((f32[8192]{0:T(1024)S(1)}, f32[8192]{0:T(1024)}, u32[]{:S(2)}) %copy-start.1) | copy-done | bytes 32792
  32.8 0.1 stack.65
  33.0 0.1 stack.66
  33.1 0.1 copy.16
  33.2 0.1 stack.67
  33.3 0.1 copy.17
  33.3 0.1 reshape.296
  33.5 0.1 stack.68
  33.6 0.1 copy.19
  33.7 0.1 stack.69
  33.9 0.1 stack.70
  34.0 0.1 copy.21
  34.0 0.1 stack.71
  34.1 0.1 copy.22
  34.2 0.1 stack.72
  34.3 0.1 copy.23
  34.4 0.1 stack.73
  34.5 0.1 copy.24
  34.5 0.1 stack.74
  34.7 0.1 stack.75
  34.8 0.1 copy.26
  34.9 0.1 stack.76
  35.1 0.1 stack.77
  35.2 0.1 copy.28
  35.2 0.1 stack.78
  35.4 0.1 stack.79
  35.6 0.1 stack.80
  35.8 0.1 stack.81
  35.9 0.6 %copy-done.6 = s32[256]{0:T(256)S(1)} copy-done((s32[256]{0:T(256)S(1)}, s32[256]{0:T(256)}, u32[]{:S(2)}) %copy-start.6) | copy-done | bytes 1048
  36.8 0.1 multiply_reduce_fusion
  36.9 0.6 %copy-done.7 = s32[256]{0:T(256)S(1)} copy-done((s32[256]{0:T(256)S(1)}, s32[256]{0:T(256)}, u32[]{:S(2)}) %copy-start.7) | copy-done | bytes 1048
  37.5 0.2 fusion.39
  37.7 2.1 %collective-permute-start = (f32[20,64]{1,0:T(8,128)S(1)}, f32[20,64]{1,0:T(8,128)S(1)}, u32[]{:S(2)}, u32[]{:S(2)}) collective-permute-start(f32[20,64]{1,0:T(8,128)S(1)} %fusion.39), channel_id=1, source_target_pairs={{0,1},{1,0},{2,3},{3,2},{4,5},{5,4},{6,7},{7,6},{8,9},{9,8},{10,11... | collective-permute-start | bytes 15368 | tf_op jit(solution)/shard_map/ppermute | solution.py:139
  39.8 1.7 %collective-permute-done = f32[20,64]{1,0:T(8,128)S(1)} collective-permute-done((f32[20,64]{1,0:T(8,128)S(1)}, f32[20,64]{1,0:T(8,128)S(1)}, u32[]{:S(2)}, u32[]{:S(2)}) %collective-permute-start) | collective-permute-done | bytes 5152 | tf_op jit(solution)/shard_map/ppermute | solution.py:139
  41.5 2.1 %collective-permute-start.1 = (f32[20,64]{1,0:T(8,128)S(1)}, f32[20,64]{1,0:T(8,128)S(1)}, u32[]{:S(2)}, u32[]{:S(2)}) collective-permute-start(f32[20,64]{1,0:T(8,128)S(1)} %add.125), channel_id=1, source_target_pairs={{0,2},{1,3},{2,0},{3,1},{4,6},{5,7},{6,4},{7,5},{8,10},{9,11},{10,... | collective-permute-start | bytes 15368 | tf_op jit(solution)/shard_map/ppermute | solution.py:139
  43.5 1.7 %collective-permute-done.1 = f32[20,64]{1,0:T(8,128)S(1)} collective-permute-done((f32[20,64]{1,0:T(8,128)S(1)}, f32[20,64]{1,0:T(8,128)S(1)}, u32[]{:S(2)}, u32[]{:S(2)}) %collective-permute-start.1) | collective-permute-done | bytes 5152 | tf_op jit(solution)/shard_map/ppermute | solution.py:139
  45.2 3.0 %collective-permute-start.2 = (f32[20,64]{1,0:T(8,128)S(1)}, f32[20,64]{1,0:T(8,128)S(1)}, u32[]{:S(2)}, u32[]{:S(2)}) collective-permute-start(f32[20,64]{1,0:T(8,128)S(1)} %add.126), channel_id=1, source_target_pairs={{0,4},{1,5},{2,6},{3,7},{4,0},{5,1},{6,2},{7,3},{8,12},{9,13},{10,... | collective-permute-start | bytes 15368 | tf_op jit(solution)/shard_map/ppermute | solution.py:139
  48.3 1.7 %collective-permute-done.2 = f32[20,64]{1,0:T(8,128)S(1)} collective-permute-done((f32[20,64]{1,0:T(8,128)S(1)}, f32[20,64]{1,0:T(8,128)S(1)}, u32[]{:S(2)}, u32[]{:S(2)}) %collective-permute-start.2) | collective-permute-done | bytes 5152 | tf_op jit(solution)/shard_map/ppermute | solution.py:139
  49.9 0.1 dynamic-slice_add_fusion
  50.2 0.6 %stack.83 = f32[5,8]{1,0:T(8,128)} concatenate(f32[1,8]{1,0:T(1,128)S(1)} %get-tuple-element.78, f32[1,8]{1,0:T(1,128)S(1)} %get-tuple-element.79, f32[1,8]{1,0:T(1,128)S(1)} %get-tuple-element.80, f32[1,8]{1,0:T(1,128)S(1)} %get-tuple-element.81, f32[1,8]{1,0:T(1,128)S(1)} %get-tuple-element.82), dimensions={0} | concatenate | bytes 320 | tf_op jit(solution)/shard_map/stack | solution.py:115
  (101 shorter events, 1.7 us)
Async XLA Ops:
  0.0 0.8 %copy-start.3 = (f32[8192]{0:T(1024)S(1)}, f32[8192]{0:T(1024)}, u32[]{:S(2)}) copy-start(f32[8192]{0:T(1024)} %param.15) | copy-start | bytes 98308
  0.8 0.7 %copy-start.5 = (f32[4,1,128]{2,1,0:T(1,128)S(1)}, f32[4,1,128]{2,1,0:T(1,128)}, u32[]{:S(2)}) copy-start(f32[4,1,128]{2,1,0:T(1,128)} %param.11) | copy-start | bytes 6148
  31.2 0.8 %copy-start = (f32[8192]{0:T(1024)S(1)}, f32[8192]{0:T(1024)}, u32[]{:S(2)}) copy-start(f32[8192]{0:T(1024)} %param.12) | copy-start | bytes 98308
  31.2 0.8 %copy-start.2 = (f32[8192]{0:T(1024)S(1)}, f32[8192]{0:T(1024)}, u32[]{:S(2)}) copy-start(f32[8192]{0:T(1024)} %param.14) | copy-start | bytes 98308
  32.0 0.8 %copy-start.1 = (f32[8192]{0:T(1024)S(1)}, f32[8192]{0:T(1024)}, u32[]{:S(2)}) copy-start(f32[8192]{0:T(1024)} %param.13) | copy-start | bytes 98308
  35.9 0.7 %copy-start.6 = (s32[256]{0:T(256)S(1)}, s32[256]{0:T(256)}, u32[]{:S(2)}) copy-start(s32[256]{0:T(256)} %param.18) | copy-start | bytes 3076
  36.8 0.7 %copy-start.7 = (s32[256]{0:T(256)S(1)}, s32[256]{0:T(256)}, u32[]{:S(2)}) copy-start(s32[256]{0:T(256)} %param.17) | copy-start | bytes 3076
  37.7 3.8 %collective-permute-start = (f32[20,64]{1,0:T(8,128)S(1)}, f32[20,64]{1,0:T(8,128)S(1)}, u32[]{:S(2)}, u32[]{:S(2)}) collective-permute-start(f32[20,64]{1,0:T(8,128)S(1)} %fusion.39), channel_id=1, source_target_pairs={{0,1},{1,0},{2,3},{3,2},{4,5},{5,4},{6,7},{7,6},{8,9},{9,8},{10,11... | collective-permute-start | bytes 15368 | tf_op jit(solution)/shard_map/ppermute | solution.py:139
  41.5 3.7 %collective-permute-start.1 = (f32[20,64]{1,0:T(8,128)S(1)}, f32[20,64]{1,0:T(8,128)S(1)}, u32[]{:S(2)}, u32[]{:S(2)}) collective-permute-start(f32[20,64]{1,0:T(8,128)S(1)} %add.125), channel_id=1, source_target_pairs={{0,2},{1,3},{2,0},{3,1},{4,6},{5,7},{6,4},{7,5},{8,10},{9,11},{10,... | collective-permute-start | bytes 15368 | tf_op jit(solution)/shard_map/ppermute | solution.py:139
  45.2 4.7 %collective-permute-start.2 = (f32[20,64]{1,0:T(8,128)S(1)}, f32[20,64]{1,0:T(8,128)S(1)}, u32[]{:S(2)}, u32[]{:S(2)}) collective-permute-start(f32[20,64]{1,0:T(8,128)S(1)} %add.126), channel_id=1, source_target_pairs={{0,4},{1,5},{2,6},{3,7},{4,0},{5,1},{6,2},{7,3},{8,12},{9,13},{10,... | collective-permute-start | bytes 15368 | tf_op jit(solution)/shard_map/ppermute | solution.py:139
  48.3 1.7 %copy-start.4 = (f32[5,8]{1,0:T(8,128)S(1)}, f32[5,8]{1,0:T(8,128)}, u32[]{:S(2)}) copy-start(f32[5,8]{1,0:T(8,128)} %param.19) | copy-start | bytes 484
